TPU v7x, 256 devices: a whole 4x4x8 slice. The times are simulated.
256 devices in a mesh: expert: 32 (over x, y, z_hi), tok: 8 (over z_lo, core).
Axes of the slice: x: 4, y: 4, z: 8 (z_hi: 2, z_lo: 4; z = z_hi * 4 + z_lo), core: 2. Of those that a mesh axis runs over, the one named last changes fastest.
Arguments:
- tokens: bfloat16 [8192, 7168], P(('tok', 'expert')), may hold values from -6 to 6
- w_gate: bfloat16 [64, 7168, 1024], P('expert', None, 'tok'), may hold values from -0.0625 to 0.0625
- w_up: bfloat16 [64, 7168, 1024], P('expert', None, 'tok'), may hold values from -0.0625 to 0.0625
- w_down: bfloat16 [64, 1024, 7168], P('expert', 'tok'), may hold values from -0.1875 to 0.1875
- gates: float32 [8, 64, 32], replicated, may hold values from 0.2 to 1
- dispatch: int32 [8, 64, 32], replicated, may hold values from 0 to 1023, as said below
Outputs:
- combined: bfloat16 [8192, 7168], P(('tok', 'expert'))
Inputs may be any that keep to these rules, and one draw needn't show every extreme that they name: `dispatch`: for each step and expert the 32 indices are different, and at most 2 of them lie in one aligned block of 32 indices (the rows of one device); in every step and for every expert some block holds exactly 2.
All inputs are finite; a program needn't handle non-finite values.
Results may differ from a plain program's by a relative error of at most 0.015.
Values may be sent and summed in bfloat16 or wider, within the bound.
A program may use at most 128 MiB of HBM per device.

v0:
```python
import jax
import jax.numpy as jnp
from jax import lax
from jax.sharding import Mesh
from jax.sharding import PartitionSpec as P

MOST = 2
TOK = ("tok_0", "tok_1")
TOK_EXPERT = ("tok_0", "tok_1", "expert")


def sum_in_order(tiles, axes, turns):
    dims = [lax.axis_size(a) for a in axes]
    tiles = tiles.reshape(*dims, *tiles.shape[1:])
    tiles = tiles.transpose(*turns, *range(len(axes), tiles.ndim))
    tiles = tiles.reshape(-1, *tiles.shape[len(axes) :])
    for k in turns:
        tiles = lax.psum_scatter(tiles, axes[k], scatter_dimension=0, tiled=True)
    return tiles[0]


def cut_along(array, dim, devices):
    before, after = (array.shape[:dim], array.shape[dim + 1 :])
    return jnp.moveaxis(array.reshape(*before, devices, -1, *after), dim, 0)


def scatter_axes(array, axes, turns, dim):
    devices = lax.axis_size(axes)
    return sum_in_order(cut_along(array, dim, devices), axes, turns)


def route_tables(dispatch, rows_dev):
    source = dispatch // rows_dev
    offset = dispatch % rows_dev
    position = jnp.arange(dispatch.shape[-1])
    earlier = (source[..., :, None] == source[..., None, :]) & (
        position[None, :] < position[:, None]
    )
    within = jnp.sum(earlier.astype(jnp.int32), axis=-1)
    return (source, offset, within)


def owner_select(source, offset, within, owner_idx, rows_dev, per_source):
    taken = (
        (source == owner_idx)[..., None] & (within[..., None] == jnp.arange(per_source))
    ).astype(jnp.bfloat16)
    row_table = (offset[..., None] == jnp.arange(rows_dev)).astype(jnp.bfloat16)
    picker = jnp.einsum("ecm,ecr->emr", taken, row_table, preferred_element_type=jnp.float32)
    return picker.astype(jnp.bfloat16).reshape(-1, rows_dev)


def slot_table(source, within, sources, per_source):
    match_source = source[..., None, None] == jnp.arange(sources)[:, None]
    match_within = within[..., None, None] == jnp.arange(per_source)[None, :]
    return (match_source & match_within).astype(jnp.bfloat16)


def expert_partial(chosen, w_gate, w_up, w_down, weight):
    gate_pre = jnp.einsum("...ecd,edh->...ech", chosen, w_gate, preferred_element_type=jnp.float32)
    up_pre = jnp.einsum("...ecd,edh->...ech", chosen, w_up, preferred_element_type=jnp.float32)
    hidden = (jax.nn.silu(gate_pre) * up_pre).astype(jnp.bfloat16)
    down_out = jnp.einsum("...ech,ehd->...ecd", hidden, w_down, preferred_element_type=jnp.float32)
    return (down_out * weight[..., None]).astype(jnp.bfloat16)


def body(tokens, w_gate, w_up, w_down, gates, dispatch):
    sources = lax.axis_size("expert")
    owners = lax.axis_size(TOK)
    rows_dev = tokens.shape[0]
    model_width = tokens.shape[1]
    exp_dev = w_gate.shape[0]
    per_source = MOST
    self_idx = lax.axis_index("expert")
    source, offset, within = route_tables(dispatch, rows_dev)
    mine_source = lax.dynamic_slice_in_dim(source, self_idx * exp_dev, exp_dev, 1)
    mine_within = lax.dynamic_slice_in_dim(within, self_idx * exp_dev, exp_dev, 1)
    gate_mine = lax.dynamic_slice_in_dim(gates, self_idx * exp_dev, exp_dev, 1)
    slots_mine = slot_table(mine_source, mine_within, sources, per_source)
    owner_idx = lax.axis_index(TOK)
    own_source = lax.dynamic_index_in_dim(source, owner_idx, 0, keepdims=False)
    own_offset = lax.dynamic_index_in_dim(offset, owner_idx, 0, keepdims=False)
    own_within = lax.dynamic_index_in_dim(within, owner_idx, 0, keepdims=False)
    picker = owner_select(own_source, own_offset, own_within, self_idx, rows_dev, per_source)
    outgoing = jnp.dot(picker, tokens, preferred_element_type=jnp.float32).astype(jnp.bfloat16)
    outgoing = outgoing.reshape(sources, exp_dev * per_source, model_width)
    arrived = lax.all_to_all(outgoing, "expert", split_axis=0, concat_axis=0, tiled=True)
    everyone = lax.all_gather(arrived[None], TOK, axis=0, tiled=True)
    everyone = everyone.reshape(owners, sources, exp_dev, per_source, model_width)
    chosen = jnp.einsum(
        "secpk,spekd->secd", slots_mine, everyone, preferred_element_type=jnp.float32
    ).astype(jnp.bfloat16)
    partial_value = expert_partial(chosen, w_gate, w_up, w_down, gate_mine)
    summed = scatter_axes(partial_value, TOK, (1, 0), 0).astype(jnp.float32)[0].astype(jnp.bfloat16)
    own_slots = lax.dynamic_index_in_dim(slots_mine, owner_idx, 0, keepdims=False)
    returning = jnp.einsum(
        "ecpk,ecd->pekd", own_slots, summed, preferred_element_type=jnp.float32
    ).astype(jnp.bfloat16)
    returning = returning.reshape(sources, exp_dev * per_source, model_width)
    returned = lax.all_to_all(returning, "expert", split_axis=0, concat_axis=0, tiled=True)
    returned = returned.reshape(sources * exp_dev * per_source, model_width)
    return jnp.dot(picker.T, returned, preferred_element_type=jnp.float32).astype(jnp.bfloat16)


def solution(mesh):
    split = Mesh(mesh.devices.reshape(mesh.shape["expert"], 4, 2), ("expert", "tok_0", "tok_1"))
    in_specs = (
        P(TOK_EXPERT, None),
        P("expert", None, TOK),
        P("expert", None, TOK),
        P("expert", TOK, None),
        P(),
        P(),
    )
    out_specs = P(TOK_EXPERT, None)
    return jax.shard_map(body, mesh=split, in_specs=in_specs, out_specs=out_specs, check_vma=False)
```

profile of v0, /device:TPU:64, one launch (start us, length us, event | category | flops | bytes accessed | tf_op | source)
XLA Modules:
  0.0 428.7 jit_solution(624430313209946607)
XLA Ops:
  6.5 1.0 add_select_fusion
  7.6 1.0 broadcast_compare_fusion
  8.6 1.2 convert_reduce_fusion
  10.0 0.5 convolution_convert_fusion.3
  10.5 1.9 convolution_convert_fusion.1
  12.3 3.1 reshape.65
  15.5 61.8 %all_to_all.10 = bf16[32,4,7168]{2,1,0:T(4,128)(2,1)S(1)} all-to-all(bf16[32,4,7168]{2,1,0:T(4,128)(2,1)S(1)} %reshape.65), channel_id=1, replica_groups=mesh['expert'=32,'tok_0'=4,'tok_1'=2] {'expert'}, dimensions={0} | all-to-all | bytes 3670016 | tf_op jit(solution)/shard_map/all_to_all | solution.py:86
  77.2 1.8 copy.57
  79.0 0.2 reduce-scatter.3.cloned.1.call-start
  79.9 0.1 iota_compare_fusion.2
  80.0 143.8 %all-gather.3.cloned.1.call-done = bf16[256,4,7168]{2,0,1:T(8,128)(2,1)} async-done(((bf16[32,4,7168]{2,0,1:T(8,128)(2,1)}), bf16[256,4,7168]{2,0,1:T(8,128)(2,1)}) %all-gather.3.cloned.1.call-update) | async-done | bytes 14680080 | tf_op jit(solution)/shard_map/all_gather | solution.py:87
  223.8 6.6 %bitcast_convert_fusion = bf16[8,2,32,7168]{3,2,1,0:T(8,128)(2,1)S(1)} fusion(bf16[8,32,2,2,7168]{4,1,0,3,2:T(8,128)(2,1)} %bitcast.74, pred[8,2,32,2]{2,3,1,0:T(4,128)(4,1)S(1)} %iota_compare_fusion.3, pred[8,2,32,32]{3,2,1,0:T(8,128)(4,1)S(1)} %iota_compare_fusion.2), kind=kOutput, calls=%fused_computation.2 | convolution fusion | flops 473464832 | bytes 22037504 | tf_op jit(solution)/shard_map/secpk,spekd->secd/dot_general | solution.py:89
  230.4 3.0 copy-done.2
  233.4 2.1 fusion.12
  235.5 12.2 %fusion = bf16[8,2,32,7168]{3,2,0,1:T(8,128)(2,1)} fusion(f32[8,2,32]{2,0,1:T(8,128)S(1)} %copy.61, bf16[2,128,7168]{2,1,0:T(8,128)(2,1)} %param.9, bf16[2,7168,128]{2,1,0:T(8,128)(2,1)} %param.8, bf16[8,2,32,7168]{3,2,1,0:T(8,128)(2,1)} %copy-done.2, f32[8,2,32,128]{3,2,0,1:T(8,128)S(1)} %fusion.12), kind=kOutput, calls=%fused_computation.1 | convolution fusion | flops 1886781440 | bytes 22284288 | tf_op jit(solution)/shard_map/...ech,ehd->...ecd/dot_general | solution.py:62
  247.7 6.7 %copy.62 = bf16[2,4,1,2,32,7168]{5,4,3,1,0,2:T(8,128)(2,1)} copy(bf16[2,4,1,2,32,7168]{5,4,0,1,3,2:T(8,128)(2,1)} %bitcast.73) | data formatting | bytes 14680064 | tf_op jit(solution)/shard_map/transpose | solution.py:15
  254.5 23.0 %reduce-scatter.3.cloned.1.call-done = bf16[4,1,2,32,7168]{4,3,2,1,0:T(8,128)(2,1)} async-done(((bf16[8,1,2,32,7168]{4,3,2,1,0:T(8,128)(2,1)}), bf16[4,1,2,32,7168]{4,3,2,1,0:T(8,128)(2,1)}) %reduce-scatter.3.cloned.1.call-update) | async-done | bytes 3670032 | tf_op jit(solution)/shard_map/reduce_scatter | solution.py:18
  277.5 0.2 broadcast_and_fusion
  277.7 77.6 %reduce-scatter.5.cloned.1.call-done = bf16[1,1,2,32,7168]{4,3,2,1,0:T(8,128)(2,1)} async-done(((bf16[4,1,2,32,7168]{4,3,2,1,0:T(8,128)(2,1)}), bf16[1,1,2,32,7168]{4,3,2,1,0:T(8,128)(2,1)}) %reduce-scatter.5.cloned.1.call-update) | async-done | bytes 917520 | tf_op jit(solution)/shard_map/reduce_scatter | solution.py:18
  355.3 1.8 convolution_convert_fusion
  357.2 1.4 copy.64
  358.6 59.4 %all_to_all.11 = bf16[32,4,7168]{2,1,0:T(4,128)(2,1)} all-to-all(bf16[32,4,7168]{2,1,0:T(4,128)(2,1)S(1)} %copy.64), channel_id=1, replica_groups=mesh['expert'=32,'tok_0'=4,'tok_1'=2] {'expert'}, dimensions={0} | all-to-all | bytes 3670016 | tf_op jit(solution)/shard_map/all_to_all | solution.py:99
  418.0 2.9 reshape.69
  421.0 1.2 convolution_convert_fusion.2
  (26 shorter events, 1.0 us)
Async XLA Ops:
  6.5 3.9 copy-start
  6.5 217.3 %all-gather.3.cloned.1.call-start = ((), (), s32[]{:S(2)}) async-start(), calls=%async_computation.6 | async-start | bytes 16515072 | tf_op jit(solution)/shard_map/all_gather | solution.py:87
  77.2 2.4 copy-start.3
  79.0 198.5 %reduce-scatter.3.cloned.1.call-start = ((), (), s32[]{:S(2)}) async-start(), calls=%async_computation.4 | async-start | bytes 11010048 | tf_op jit(solution)/shard_map/reduce_scatter | solution.py:18
  223.8 9.6 %copy-start.4 = (bf16[2,7168,128]{2,1,0:T(8,128)(2,1)S(1)}, bf16[2,7168,128]{2,1,0:T(8,128)(2,1)}, u32[]{:S(2)}) copy-start(bf16[2,7168,128]{2,1,0:T(8,128)(2,1)} %param.7) | copy-start | bytes 11010052
  230.4 3.0 copy-start.2
  254.4 100.9 %reduce-scatter.5.cloned.1.call-start = ((), (), s32[]{:S(2)}) async-start(), calls=%async_computation.5 | async-start | bytes 4587520 | tf_op jit(solution)/shard_map/reduce_scatter | solution.py:18
  358.6 63.5 %copy-start.1 = (bf16[32,7168]{1,0:T(8,128)(2,1)S(1)}, bf16[32,7168]{1,0:T(8,128)(2,1)}, u32[]{:S(2)}) copy-start(bf16[32,7168]{1,0:T(8,128)(2,1)} %param.6) | copy-start | bytes 1376260
Sparse Core Ops, SparseCore 0:
  79.2 144.5 all-gather.2
  254.6 22.8 reduce-scatter.2
  280.1 75.2 reduce-scatter.4
where the time goes:
time: 429 us
  waiting for transfers between devices  244 us (57%)
  blocking collectives  121 us (28%)
  matrix products  26.2 us (6%)
  local copies, waits for them, and re-layouts  19.8 us (5%)
  between operations  13.3 us (3%)
    all_gather x1, waiting for transfers between devices, body(): everyone = lax.all_gather(arrived[None], TOK, axis=0, tiled=True)  144 us
    reduce_scatter x2, waiting for transfers between devices, sum_in_order(): tiles = lax.psum_scatter(tiles, axes[k], scatter_dimension=0, tiled=True)  101 us
    all_to_all x1, blocking collectives, body(): lax.all_to_all(outgoing, 'expert', split_axis=0, concat_axis=0, tiled=True)  61.8 us
    all_to_all x1, blocking collectives, body(): lax.all_to_all(returning, 'expert', split_axis=0, concat_axis=0, tiled=True)  59.4 us
    dot_general x1, matrix products, expert_partial(): jnp.einsum('...ech,ehd->...ecd', hidden, w_down, preferred_element_type=j...  12.2 us
  transfers between devices with their start and end apart: 3, of which 3 were waited for; matrix products, arithmetic and copies ran while one was open for 0% of the time, Pallas kernels for 0%

commit v1 on v0

--- a/solution.py
+++ b/solution.py
@@ -84,7 +84,9 @@
     outgoing = jnp.dot(picker, tokens, preferred_element_type=jnp.float32).astype(jnp.bfloat16)
     outgoing = outgoing.reshape(sources, exp_dev * per_source, model_width)
     arrived = lax.all_to_all(outgoing, "expert", split_axis=0, concat_axis=0, tiled=True)
-    everyone = lax.all_gather(arrived[None], TOK, axis=0, tiled=True)
+    everyone = jnp.concatenate(
+        lax.all_to_all(jnp.stack([arrived[None]] * lax.axis_size(TOK)), TOK, 0, 0), axis=0
+    )
     everyone = everyone.reshape(owners, sources, exp_dev, per_source, model_width)
     chosen = jnp.einsum(
         "secpk,spekd->secd", slots_mine, everyone, preferred_element_type=jnp.float32

time: 429 us -> 606 us (1.41)
  waiting for transfers between devices: 244 us -> 409 us
  starting transfers between devices: 0.27 us -> 6.37 us
    all_to_all x0 -> x1, waiting for transfers between devices: none -> 315 us  [body(): lax.all_to_all(jnp.stack([arrived[None]] * lax.axis_size(TOK)), TOK, 0, 0)]
    all_gather x1 -> x0, waiting for transfers between devices: 144 us -> none  [body(): everyone = lax.all_gather(arrived[None], TOK, axis=0, tiled=True)]
    all_to_all x0 -> x1, starting transfers between devices: none -> 6.32 us  [body(): lax.all_to_all(jnp.stack([arrived[None]] * lax.axis_size(TOK)), TOK, 0, 0)]
where the time goes in v1:
time: 606 us; the launch traced here: 605 us
  waiting for transfers between devices  409 us (67%)
  blocking collectives  121 us (20%)
  matrix products  27.1 us (4%)
  local copies, waits for them, and re-layouts  24.1 us (4%)
  between operations  13.6 us (2%)
  starting transfers between devices  6.37 us (1%)
    all_to_all x1, waiting for transfers between devices, body(): lax.all_to_all(jnp.stack([arrived[None]] * lax.axis_size(TOK)), TOK, 0, 0)  315 us
    reduce_scatter x2, waiting for transfers between devices, sum_in_order(): tiles = lax.psum_scatter(tiles, axes[k], scatter_dimension=0, tiled=True)  94.8 us
    all_to_all x1, blocking collectives, body(): lax.all_to_all(outgoing, 'expert', split_axis=0, concat_axis=0, tiled=True)  61.8 us
    all_to_all x1, blocking collectives, body(): lax.all_to_all(returning, 'expert', split_axis=0, concat_axis=0, tiled=True)  59.4 us
    dot_general x1, matrix products, expert_partial(): jnp.einsum('...ech,ehd->...ecd', hidden, w_down, preferred_element_type=j...  12.2 us
  transfers between devices with their start and end apart: 3, of which 3 were waited for; matrix products, arithmetic and copies ran while one was open for 0% of the time, Pallas kernels for 0%

profile of v1, /device:TPU:64, one launch (start us, length us, event | category | flops | bytes accessed | tf_op | source)
XLA Modules:
  0.0 605.3 jit_solution(17813312646963426684)
XLA Ops:
  6.5 1.0 broadcast_compare_fusion
  7.6 1.0 add_select_fusion
  8.7 1.2 convert_reduce_fusion
  10.0 0.5 convolution_convert_fusion.3
  10.5 1.9 convolution_convert_fusion.1
  12.3 3.1 reshape.64
  15.5 61.8 %all_to_all.15 = bf16[32,4,7168]{2,1,0:T(4,128)(2,1)S(1)} all-to-all(bf16[32,4,7168]{2,1,0:T(4,128)(2,1)S(1)} %reshape.64), channel_id=1, replica_groups=mesh['expert'=32,'tok_0'=4,'tok_1'=2] {'expert'}, dimensions={0} | all-to-all | bytes 3670016 | tf_op jit(solution)/shard_map/all_to_all | solution.py:86
  77.2 0.5 copy.55
  77.8 5.5 stack.3
  83.3 6.3 %all-to-all-start.1 = ((bf16[8,1,32,4,7168]{4,2,3,1,0:T(8,128)(2,1)}), bf16[8,1,32,4,7168]{4,2,3,1,0:T(8,128)(2,1)}, u32[]{:S(2)}, u32[]{:S(2)}) async-start(bf16[8,1,32,4,7168]{4,2,3,1,0:T(8,128)(2,1)} %stack.3), calls=%async_computation.1 | async-start | bytes 29360128 | tf_op jit(solution)/shard_map/all_to_all | solution.py:88
  90.4 314.6 %all-to-all-done.1 = bf16[8,1,32,4,7168]{4,2,3,1,0:T(8,128)(2,1)} async-done(((bf16[8,1,32,4,7168]{4,2,3,1,0:T(8,128)(2,1)}), bf16[8,1,32,4,7168]{4,2,3,1,0:T(8,128)(2,1)}, u32[]{:S(2)}, u32[]{:S(2)}) %all-to-all-start.1) | async-done | bytes 14680096 | tf_op jit(solution)/shard_map/all_to_all | solution.py:88
  405.0 7.5 %bitcast_convert_fusion = bf16[8,2,32,7168]{3,2,1,0:T(8,128)(2,1)S(1)} fusion(bf16[8,32,2,2,7168]{4,1,3,2,0:T(8,128)(2,1)} %bitcast.4, pred[8,2,32,2]{2,3,1,0:T(4,128)(4,1)S(1)} %iota_compare_fusion.3, pred[8,2,32,32]{3,2,1,0:T(8,128)(4,1)S(1)} %iota_compare_fusion.2), kind=kOutput, calls=%fused_computation.2 | convolution fusion | flops 473464832 | bytes 22037504 | tf_op jit(solution)/shard_map/secpk,spekd->secd/dot_general | solution.py:91
  412.6 3.0 copy-done.2
  415.6 2.1 fusion.8
  417.6 12.2 %fusion = bf16[8,2,32,7168]{3,2,0,1:T(8,128)(2,1)} fusion(f32[8,2,32]{2,0,1:T(8,128)S(1)} %copy.58, bf16[2,128,7168]{2,1,0:T(8,128)(2,1)} %param.9, bf16[2,7168,128]{2,1,0:T(8,128)(2,1)} %param.8, bf16[8,2,32,7168]{3,2,1,0:T(8,128)(2,1)} %copy-done.2, f32[8,2,32,128]{3,2,0,1:T(8,128)S(1)} %fusion.8), kind=kOutput, calls=%fused_computation.1 | convolution fusion | flops 1886781440 | bytes 22284288 | tf_op jit(solution)/shard_map/...ech,ehd->...ecd/dot_general | solution.py:62
  429.8 6.7 %copy.59 = bf16[2,4,1,2,32,7168]{5,4,3,1,0,2:T(8,128)(2,1)} copy(bf16[2,4,1,2,32,7168]{5,4,0,1,3,2:T(8,128)(2,1)} %bitcast.74) | data formatting | bytes 14680064 | tf_op jit(solution)/shard_map/transpose | solution.py:15
  436.6 17.2 %reduce-scatter.3.cloned.1.call-done = bf16[4,1,2,32,7168]{4,3,2,1,0:T(8,128)(2,1)} async-done(((bf16[8,1,2,32,7168]{4,3,2,1,0:T(8,128)(2,1)}), bf16[4,1,2,32,7168]{4,3,2,1,0:T(8,128)(2,1)}) %reduce-scatter.3.cloned.1.call-update) | async-done | bytes 3670032 | tf_op jit(solution)/shard_map/reduce_scatter | solution.py:18
  453.9 0.2 broadcast_and_fusion
  454.1 77.6 %reduce-scatter.5.cloned.1.call-done = bf16[1,1,2,32,7168]{4,3,2,1,0:T(8,128)(2,1)} async-done(((bf16[4,1,2,32,7168]{4,3,2,1,0:T(8,128)(2,1)}), bf16[1,1,2,32,7168]{4,3,2,1,0:T(8,128)(2,1)}) %reduce-scatter.5.cloned.1.call-update) | async-done | bytes 917520 | tf_op jit(solution)/shard_map/reduce_scatter | solution.py:18
  531.7 1.9 convolution_convert_fusion
  533.5 1.4 copy.61
  535.0 59.4 %all_to_all.16 = bf16[32,4,7168]{2,1,0:T(4,128)(2,1)} all-to-all(bf16[32,4,7168]{2,1,0:T(4,128)(2,1)S(1)} %copy.61), channel_id=1, replica_groups=mesh['expert'=32,'tok_0'=4,'tok_1'=2] {'expert'}, dimensions={0} | all-to-all | bytes 3670016 | tf_op jit(solution)/shard_map/all_to_all | solution.py:101
  594.3 2.9 reshape.67
  597.3 1.2 convolution_convert_fusion.2
  (26 shorter events, 1.1 us)
Async XLA Ops:
  6.5 3.9 copy-start
  83.3 6.3 %copy-start.3 = (f32[8,64,32]{1,2,0:T(8,128)S(1)}, f32[8,64,32]{1,2,0:T(8,128)}, u32[]{:S(2)}) copy-start(f32[8,64,32]{1,2,0:T(8,128)} %param.10) | copy-start | bytes 196612
  83.3 321.7 %all-to-all-start.1 = ((bf16[8,1,32,4,7168]{4,2,3,1,0:T(8,128)(2,1)}), bf16[8,1,32,4,7168]{4,2,3,1,0:T(8,128)(2,1)}, u32[]{:S(2)}, u32[]{:S(2)}) async-start(bf16[8,1,32,4,7168]{4,2,3,1,0:T(8,128)(2,1)} %stack.3), calls=%async_computation.1 | async-start | bytes 29360128 | tf_op jit(solution)/shard_map/all_to_all | solution.py:88
  89.6 364.2 %reduce-scatter.3.cloned.1.call-start = ((), (), s32[]{:S(2)}) async-start(), calls=%async_computation.5 | async-start | bytes 11010048 | tf_op jit(solution)/shard_map/reduce_scatter | solution.py:18
  405.0 10.6 %copy-start.4 = (bf16[2,7168,128]{2,1,0:T(8,128)(2,1)S(1)}, bf16[2,7168,128]{2,1,0:T(8,128)(2,1)}, u32[]{:S(2)}) copy-start(bf16[2,7168,128]{2,1,0:T(8,128)(2,1)} %param.7) | copy-start | bytes 11010052
  412.6 3.0 copy-start.2
  436.6 95.1 %reduce-scatter.5.cloned.1.call-start = ((), (), s32[]{:S(2)}) async-start(), calls=%async_computation.6 | async-start | bytes 4587520 | tf_op jit(solution)/shard_map/reduce_scatter | solution.py:18
  534.9 63.5 %copy-start.1 = (bf16[32,7168]{1,0:T(8,128)(2,1)S(1)}, bf16[32,7168]{1,0:T(8,128)(2,1)}, u32[]{:S(2)}) copy-start(bf16[32,7168]{1,0:T(8,128)(2,1)} %param.6) | copy-start | bytes 1376260
Sparse Core Ops, SparseCore 0:
  436.7 17.1 reduce-scatter.2
  456.4 75.2 reduce-scatter.4
